TPU v7x, 8 devices: a whole 2x2x1 slice. The times are simulated.
8 devices in a mesh: dp: 1 (over z), a: 2 (over y), b: 4 (over x, core).
Axes of the slice: x: 2, y: 2, z: 1, core: 2. Of those that a mesh axis runs over, the one named last changes fastest.
Arguments:
- x: bfloat16 [2048, 8192], P('dp', ('a', 'b'))
- w_gate: bfloat16 [8192, 32768], P('a', 'b')
- w_up: bfloat16 [8192, 32768], P('a', 'b')
- w_down: bfloat16 [32768, 8192], P('b', 'a')
Outputs:
- output: bfloat16 [2048, 8192], P('dp', ('a', 'b'))
All inputs are finite; a program needn't handle non-finite values.
Results may differ from a plain program's by a relative error of at most 0.016.
Values are sent between devices in bfloat16 or wider.
A program may use at most 2 GiB of HBM per device.

v0:
```python
import jax
import jax.numpy as jnp


def solution(mesh):
    def step(x, w_gate, w_up, w_down):
        gate, up = jnp.dot(x, w_gate), jnp.dot(x, w_up)
        hidden = (jax.nn.silu(gate.astype(jnp.float32)) * up.astype(jnp.float32)).astype(jnp.bfloat16)
        return jnp.dot(hidden, w_down)

    return step
```

profile of v0, /device:TPU:1, one launch (start us, length us, event | category | flops | bytes accessed | tf_op | source)
XLA Modules:
  0.0 2164.7 jit_solution(1016923304962726310)
XLA Ops:
  6.5 0.0 all-gather.4.cloned.1.call-start
  6.5 0.7 all-gather.4.cloned.1.call-update
  7.3 0.0 all-reduce.7.cloned.1.call-start
  7.3 108.0 %all-gather.4.cloned.1.call-done = bf16[2048,4096]{1,0:T(8,128)(2,1)} async-done(((bf16[2048,1024]{1,0:T(8,128)(2,1)}), bf16[2048,4096]{1,0:T(8,128)(2,1)}) %all-gather.4.cloned.1.call-update) | async-done | bytes 16777232 | tf_op args[0]
  115.3 151.1 %fusion.9 = bf16[2048,8192]{1,0:T(8,128)(2,1)} fusion(bf16[2048,4096]{1,0:T(8,128)(2,1)} %all-gather.4.cloned.1.call-done, bf16[4096,8192]{1,0:T(8,128)(2,1)} %param.2), kind=kOutput, calls=%fused_computation.10 | convolution fusion | flops 137438953472 | bytes 117440512 | tf_op jit(solution)/dot_general | solution.py:7
  266.4 161.3 %fusion.8 = bf16[2048,8192]{1,0:T(8,128)(2,1)} fusion(bf16[2048,4096]{1,0:T(8,128)(2,1)} %all-gather.4.cloned.1.call-done, bf16[4096,8192]{1,0:T(8,128)(2,1)} %param.1), kind=kOutput, calls=%fused_computation.9 | convolution fusion | flops 137438953472 | bytes 117440512 | tf_op jit(solution)/dot_general | solution.py:7
  427.8 0.0 all-reduce.7.cloned.1.call-update
  427.8 0.0 reduce-scatter.4.cloned.1.call-start
  427.8 1451.2 %all-reduce.7.cloned.1.call-done = (bf16[2048,8192]{1,0:T(8,128)(2,1)}, bf16[2048,8192]{1,0:T(8,128)(2,1)}) async-done(((bf16[2048,8192]{1,0:T(8,128)(2,1)}, bf16[2048,8192]{1,0:T(8,128)(2,1)}), (bf16[2048,8192]{1,0:T(8,128)(2,1)}, bf16[2048,8192]{1,0:T(8,128)(2,1)})) %all-reduce.7.cloned.1.call-update) | async-done | bytes 67108880 | tf_op jit(solution)/dot_general | solution.py:7
  1879.0 157.9 %fusion.5 = bf16[2048,4096]{1,0:T(8,128)(2,1)} fusion(bf16[8192,4096]{1,0:T(8,128)(2,1)} %param.3, bf16[2048,8192]{1,0:T(8,128)(2,1)} %get-tuple-element.4, bf16[2048,8192]{1,0:T(8,128)(2,1)} %get-tuple-element.5), kind=kOutput, calls=%fused_computation.7 | convolution fusion | flops 137573171200 | bytes 150994944 | tf_op jit(solution)/dot_general | solution.py:9
  2036.9 0.0 reduce-scatter.4.cloned.1.call-update
  2036.9 120.8 %reduce-scatter.4.cloned.1.call-done = bf16[2048,1024]{1,0:T(8,128)(2,1)} async-done(((bf16[2048,4096]{1,0:T(8,128)(2,1)}), bf16[2048,1024]{1,0:T(8,128)(2,1)}) %reduce-scatter.4.cloned.1.call-update) | async-done | bytes 4194320
Async XLA Ops:
  6.5 108.8 %all-gather.4.cloned.1.call-start = ((), (), s32[]{:S(2)}) async-start(), calls=%async_computation.1 | async-start | bytes 20971520 | tf_op args[0]
  7.3 1871.7 %all-reduce.7.cloned.1.call-start = ((), (), s32[]{:S(2)}) async-start(), calls=%async_computation.3 | async-start | bytes 134217728 | tf_op jit(solution)/dot_general | solution.py:7
  427.8 1730.0 %reduce-scatter.4.cloned.1.call-start = ((), (), s32[]{:S(2)}) async-start(), calls=%async_computation.2 | async-start | bytes 20971520
Sparse Core Ops, SparseCore 0:
  8.9 106.3 all-gather.3
  427.9 1451.0 all-reduce.6
  2037.1 120.6 reduce-scatter.3
where the time goes:
time: 2170 us; the launch traced here: 2160 us
  waiting for transfers between devices  1680 us (77%)
  matrix products  470 us (22%)
    dot_general x1, waiting for transfers between devices, step(): gate, up = (jnp.dot(x, w_gate), jnp.dot(x, w_up))  1450 us
    dot_general x2, matrix products, step(): gate, up = (jnp.dot(x, w_gate), jnp.dot(x, w_up))  312 us
    unnamed x5, waiting for transfers between devices  230 us
    dot_general x1, matrix products, step(): return jnp.dot(hidden, w_down)  158 us
  transfers between devices with their start and end apart: 3, of which 3 were waited for; matrix products, arithmetic and copies ran while one was open for 0% of the time, Pallas kernels for 0%

commit v1 on v0

v1 whole, which is shorter than its diff:
```python
import jax
import jax.numpy as jnp
from jax import lax
from jax.sharding import PartitionSpec as P

CHUNKS = (512, 1024, 512)


def solution(mesh):
    swap = [(0, 1), (1, 0)]

    def body(x, wg, wu, wd):
        mine = lax.axis_index("a")
        outs = []
        start = 0
        for rows in CHUNKS:
            half = rows // 2
            xc = lax.all_gather(x[start : start + rows], "b", axis=1, tiled=True)
            xt = lax.dynamic_slice_in_dim(xc, (1 - mine) * half, half, 0)
            xm = lax.dynamic_slice_in_dim(xc, mine * half, half, 0)
            gt = lax.ppermute(jnp.dot(xt, wg), "a", swap)
            ut = lax.ppermute(jnp.dot(xt, wu), "a", swap)
            gm = jnp.dot(xm, wg, preferred_element_type=jnp.float32)
            um = jnp.dot(xm, wu, preferred_element_type=jnp.float32)
            g = gm + gt.astype(jnp.float32)
            u = um + ut.astype(jnp.float32)
            h = (jax.nn.silu(g) * u).astype(jnp.bfloat16)
            ht = lax.ppermute(h, "a", swap)
            ym = jnp.dot(h, wd)
            yt = jnp.dot(ht, wd)
            lo = jnp.where(mine == 0, ym, yt)
            hi = jnp.where(mine == 0, yt, ym)
            y = jnp.concatenate([lo, hi], 0)
            outs.append(lax.psum_scatter(y, "b", scatter_dimension=1, tiled=True))
            start += rows
        return jnp.concatenate(outs, 0)

    return jax.shard_map(
        body,
        mesh=mesh,
        in_specs=(P("dp", ("a", "b")), P("a", "b"), P("a", "b"), P("b", "a")),
        out_specs=P("dp", ("a", "b")),
        check_vma=False,
    )
```

time: 2170 us -> 1380 us (0.64)
  waiting for transfers between devices: 1680 us -> 699 us
  matrix products: 470 us -> 628 us
    dot_general x1 -> x0, waiting for transfers between devices: 1450 us -> none  [step(): gate, up = (jnp.dot(x, w_gate), jnp.dot(x, w_up))]
    ppermute x0 -> x9, waiting for transfers between devices: none -> 601 us  [the longest x3 270 us: body(): ut = lax.ppermute(jnp.dot(xt, wu), 'a', swap)]
    unnamed x5 -> x6, waiting for transfers between devices: 230 us -> 0.78 us
    dot_general x3 -> x18, matrix products: 470 us -> 628 us  [the longest x3 117 us: body(): gm = jnp.dot(xm, wg, preferred_element_type=jnp.float32)]
    reduce_scatter x0 -> x3, waiting for transfers between devices: none -> 66.9 us  [body(): outs.append(lax.psum_scatter(y, 'b', scatter_dimension=1, tiled=True))]
    all_gather x0 -> x3, waiting for transfers between devices: none -> 29.9 us  [body(): xc = lax.all_gather(x[start:start + rows], 'b', axis=1, tiled=True)]
  transfers between devices with their start and end apart: 3 -> 15, of which waited for: 3 -> 7; matrix products, arithmetic and copies ran while one was open for 0% -> 47% of each run, Pallas kernels for 0% -> 0%
where the time goes in v1:
time: 1380 us; the launch traced here: 1370 us
  waiting for transfers between devices  699 us (51%)
  matrix products  628 us (46%)
  other arithmetic  16.5 us (1%)
  between operations  14 us (1%)
    ppermute x3, waiting for transfers between devices, body(): ut = lax.ppermute(jnp.dot(xt, wu), 'a', swap)  270 us
    ppermute x3, waiting for transfers between devices, body(): gt = lax.ppermute(jnp.dot(xt, wg), 'a', swap)  227 us
    dot_general x3, matrix products, body(): gm = jnp.dot(xm, wg, preferred_element_type=jnp.float32)  117 us
    dot_general x3, matrix products, body(): um = jnp.dot(xm, wu, preferred_element_type=jnp.float32)  107 us
    ppermute x3, waiting for transfers between devices, body(): ht = lax.ppermute(h, 'a', swap)  105 us
    dot_general x3, matrix products, body(): ut = lax.ppermute(jnp.dot(xt, wu), 'a', swap)  102 us
    dot_general x3, matrix products, body(): gt = lax.ppermute(jnp.dot(xt, wg), 'a', swap)  102 us
    dot_general x3, matrix products, body(): ym = jnp.dot(h, wd)  101 us
  transfers between devices with their start and end apart: 15, of which 7 were waited for; matrix products, arithmetic and copies ran while one was open for 47% of the time, Pallas kernels for 0%

profile of v1, /device:TPU:1, one launch (start us, length us, event | category | flops | bytes accessed | tf_op | source)
XLA Modules:
  0.0 1370.2 jit_solution(6171482231834593002)
XLA Ops:
  13.6 29.9 %all-gather.4.cloned.1.call-done = bf16[512,4096]{1,0:T(8,128)(2,1)} async-done(((bf16[512,1024]{1,0:T(8,128)(2,1)}), bf16[512,4096]{1,0:T(8,128)(2,1)}) %all-gather.4.cloned.1.call-update) | async-done | bytes 4194320 | tf_op jit(solution)/shard_map/all_gather | solution.py:18
  43.5 29.1 %fusion.22 = bf16[256,8192]{1,0:T(8,128)(2,1)} fusion(bf16[4096,8192]{1,0:T(8,128)(2,1)} %param.5, bf16[512,4096]{1,0:T(8,128)(2,1)} %all-gather.4.cloned.1.call-done, s32[]{:T(128)S(6)} %select_n.48), kind=kOutput, calls=%fused_computation.31 | convolution fusion | flops 17179869184 | bytes 73400320 | tf_op jit(solution)/shard_map/dot_general | solution.py:21
  73.8 29.1 %fusion.20 = bf16[256,8192]{1,0:T(8,128)(2,1)} fusion(bf16[4096,8192]{1,0:T(8,128)(2,1)} %param.6, bf16[512,4096]{1,0:T(8,128)(2,1)} %all-gather.4.cloned.1.call-done, s32[]{:T(128)S(6)} %select_n.48), kind=kOutput, calls=%fused_computation.29 | convolution fusion | flops 17179869184 | bytes 73400320 | tf_op jit(solution)/shard_map/dot_general | solution.py:22
  103.2 29.3 %fusion.12 = bf16[256,8192]{1,0:T(8,128)(2,1)} fusion(bf16[4096,8192]{1,0:T(8,128)(2,1)} %param.5, bf16[512,4096]{1,0:T(8,128)(2,1)} %all-gather.8.cloned.1.call-done, s32[]{:T(128)S(6)} %select_n.48), kind=kOutput, calls=%fused_computation.23 | convolution fusion | flops 17179869184 | bytes 73400320 | tf_op jit(solution)/shard_map/dot_general | solution.py:21
  133.6 29.0 %fusion.10 = bf16[256,8192]{1,0:T(8,128)(2,1)} fusion(bf16[4096,8192]{1,0:T(8,128)(2,1)} %param.6, bf16[512,4096]{1,0:T(8,128)(2,1)} %all-gather.8.cloned.1.call-done, s32[]{:T(128)S(6)} %select_n.48), kind=kOutput, calls=%fused_computation.21 | convolution fusion | flops 17179869184 | bytes 73400320 | tf_op jit(solution)/shard_map/dot_general | solution.py:22
  162.9 31.4 %fusion.14 = f32[256,8192]{1,0:T(8,128)} fusion(bf16[4096,8192]{1,0:T(8,128)(2,1)} %param.6, bf16[512,4096]{1,0:T(8,128)(2,1)} %all-gather.8.cloned.1.call-done, s32[]{:T(128)S(6)} %select_n.47), kind=kOutput, calls=%fused_computation.25 | convolution fusion | flops 17179869184 | bytes 77594624 | tf_op jit(solution)/shard_map/dot_general | solution.py:24
  194.4 31.0 %fusion.24 = f32[256,8192]{1,0:T(8,128)} fusion(bf16[4096,8192]{1,0:T(8,128)(2,1)} %param.6, bf16[512,4096]{1,0:T(8,128)(2,1)} %all-gather.4.cloned.1.call-done, s32[]{:T(128)S(6)} %select_n.47), kind=kOutput, calls=%fused_computation.33 | convolution fusion | flops 17179869184 | bytes 77594624 | tf_op jit(solution)/shard_map/dot_general | solution.py:24
  225.4 118.9 %collective-permute-done.6 = bf16[256,8192]{1,0:T(8,128)(2,1)} collective-permute-done((bf16[256,8192]{1,0:T(8,128)(2,1)}, bf16[256,8192]{1,0:T(8,128)(2,1)}, u32[]{:S(2)}, u32[]{:S(2)}) %collective-permute-start.6) | collective-permute-done | bytes 4194336 | tf_op jit(solution)/shard_map/ppermute | solution.py:21
  344.3 89.9 %collective-permute-done.7 = bf16[256,8192]{1,0:T(8,128)(2,1)} collective-permute-done((bf16[256,8192]{1,0:T(8,128)(2,1)}, bf16[256,8192]{1,0:T(8,128)(2,1)}, u32[]{:S(2)}, u32[]{:S(2)}) %collective-permute-start.7) | collective-permute-done | bytes 4194336 | tf_op jit(solution)/shard_map/ppermute | solution.py:22
  434.2 33.2 %multiply_convert_fusion.1 = bf16[256,8192]{1,0:T(8,128)(2,1)} fusion(f32[256,8192]{1,0:T(8,128)} %fusion.14, bf16[256,8192]{1,0:T(8,128)(2,1)} %collective-permute-done.7, bf16[256,8192]{1,0:T(8,128)(2,1)} %collective-permute-done.6, bf16[4096,8192]{1,0:T(8,128)(2,1)} %param.5, bf16[512,4096]{1,0:T(8,128)(2,1)} %all-gather.8.cloned.1.call-done, ...), kind=kOutput, calls=%fused_computation.2 | convolution fusion | flops 17200840704 | bytes 90177536 | tf_op jit(solution)/shard_map/dot_general | solution.py:23
  468.6 33.1 %multiply_convert_fusion.2 = bf16[256,8192]{1,0:T(8,128)(2,1)} fusion(f32[256,8192]{1,0:T(8,128)} %fusion.24, bf16[256,8192]{1,0:T(8,128)(2,1)} %collective-permute-done.1, bf16[256,8192]{1,0:T(8,128)(2,1)} %collective-permute-done, bf16[4096,8192]{1,0:T(8,128)(2,1)} %param.5, bf16[512,4096]{1,0:T(8,128)(2,1)} %all-gather.4.cloned.1.call-done, s32[]{:T(128)S(6)} %select_n.47), kind=kOutput, calls=%fused_computation.3 | convolution fusion | flops 17200840704 | bytes 90177536 | tf_op jit(solution)/shard_map/dot_general | solution.py:23
  501.9 28.3 %fusion.45 = bf16[256,4096]{1,0:T(8,128)(2,1)} fusion(bf16[256,8192]{1,0:T(8,128)(2,1)} %multiply_convert_fusion.1, bf16[8192,4096]{1,0:T(8,128)(2,1)} %param.7), kind=kOutput, calls=%fused_computation.52 | convolution fusion | flops 17179869184 | bytes 73400320 | tf_op jit(solution)/shard_map/dot_general | solution.py:29
  530.2 27.5 %fusion.43 = bf16[256,4096]{1,0:T(8,128)(2,1)} fusion(bf16[256,8192]{1,0:T(8,128)(2,1)S(1)} %copy-done, bf16[8192,4096]{1,0:T(8,128)(2,1)} %param.7), kind=kOutput, calls=%fused_computation.50 | convolution fusion | flops 17179869184 | bytes 73400320 | tf_op jit(solution)/shard_map/dot_general | solution.py:29
  557.7 43.6 %fusion.2 = bf16[512,8192]{1,0:T(8,128)(2,1)} fusion(bf16[4096,8192]{1,0:T(8,128)(2,1)} %param.5, bf16[1024,4096]{1,0:T(8,128)(2,1)} %all-gather.6.cloned.1.call-done, s32[]{:T(128)S(6)} %select_n.53), kind=kOutput, calls=%fused_computation.11 | convolution fusion | flops 34359738368 | bytes 79691776 | tf_op jit(solution)/shard_map/dot_general | solution.py:21
  602.2 44.0 %fusion = bf16[512,8192]{1,0:T(8,128)(2,1)} fusion(bf16[4096,8192]{1,0:T(8,128)(2,1)} %param.6, bf16[1024,4096]{1,0:T(8,128)(2,1)} %all-gather.6.cloned.1.call-done, s32[]{:T(128)S(6)} %select_n.53), kind=kOutput, calls=%fused_computation.9 | convolution fusion | flops 34359738368 | bytes 79691776 | tf_op jit(solution)/shard_map/dot_general | solution.py:22
  646.7 44.3 %fusion.4 = f32[512,8192]{1,0:T(8,128)} fusion(bf16[4096,8192]{1,0:T(8,128)(2,1)} %param.6, bf16[1024,4096]{1,0:T(8,128)(2,1)} %all-gather.6.cloned.1.call-done, s32[]{:T(128)S(6)} %select_n.52), kind=kOutput, calls=%fused_computation.13 | convolution fusion | flops 34359738368 | bytes 88080384 | tf_op jit(solution)/shard_map/dot_general | solution.py:24
  691.0 27.1 %broadcast_select_fusion.3 = (bf16[256,4096]{1,0:T(8,128)(2,1)S(1)}, bf16[256,4096]{1,0:T(8,128)(2,1)S(1)}) fusion(bf16[256,4096]{1,0:T(8,128)(2,1)S(1)} %copy-done.2, pred[]{:T(512)S(6)} %eq.2, bf16[256,8192]{1,0:T(8,128)(2,1)} %collective-permute-done.8, bf16[8192,4096]{1,0:T(8,128)(2,1)} %param.7), kind=kOutput, calls=%fused_computation.18 | convolution fusion | flops 17181966336 | bytes 77594624 | tf_op jit(solution)/shard_map/dot_general | solution.py:30
  720.7 107.6 %collective-permute-done.3 = bf16[512,8192]{1,0:T(8,128)(2,1)} collective-permute-done((bf16[512,8192]{1,0:T(8,128)(2,1)}, bf16[512,8192]{1,0:T(8,128)(2,1)}, u32[]{:S(2)}, u32[]{:S(2)}) %collective-permute-start.3) | collective-permute-done | bytes 8388640 | tf_op jit(solution)/shard_map/ppermute | solution.py:21
  828.3 179.8 %collective-permute-done.4 = bf16[512,8192]{1,0:T(8,128)(2,1)} collective-permute-done((bf16[512,8192]{1,0:T(8,128)(2,1)}, bf16[512,8192]{1,0:T(8,128)(2,1)}, u32[]{:S(2)}, u32[]{:S(2)}) %collective-permute-start.4) | collective-permute-done | bytes 8388640 | tf_op jit(solution)/shard_map/ppermute | solution.py:22
  1008.0 50.7 %multiply_convert_fusion = bf16[512,8192]{1,0:T(8,128)(2,1)} fusion(f32[512,8192]{1,0:T(8,128)} %fusion.4, bf16[512,8192]{1,0:T(8,128)(2,1)} %collective-permute-done.4, bf16[512,8192]{1,0:T(8,128)(2,1)} %collective-permute-done.3, bf16[4096,8192]{1,0:T(8,128)(2,1)} %param.5, bf16[1024,4096]{1,0:T(8,128)(2,1)} %all-gather.6.cloned.1.call-done, s32[]{:T(128)S(6)} %select_n.52), kind=kOutput, calls=%fused_computation | convolution fusion | flops 34401681408 | bytes 113246208 | tf_op jit(solution)/shard_map/dot_general | solution.py:23
  1089.4 44.7 %fusion.44 = bf16[512,4096]{1,0:T(8,128)(2,1)} fusion(bf16[512,8192]{1,0:T(8,128)(2,1)} %multiply_convert_fusion, bf16[8192,4096]{1,0:T(8,128)(2,1)} %param.7), kind=kOutput, calls=%fused_computation.51 | convolution fusion | flops 34359738368 | bytes 79691776 | tf_op jit(solution)/shard_map/dot_general | solution.py:29
  1134.1 105.0 %collective-permute-done.5 = bf16[512,8192]{1,0:T(8,128)(2,1)} collective-permute-done((bf16[512,8192]{1,0:T(8,128)(2,1)}, bf16[512,8192]{1,0:T(8,128)(2,1)}, u32[]{:S(2)}, u32[]{:S(2)}) %collective-permute-start.5) | collective-permute-done | bytes 8388640 | tf_op jit(solution)/shard_map/ppermute | solution.py:28
  1239.1 45.4 %broadcast_select_fusion.1 = (bf16[512,4096]{1,0:T(8,128)(2,1)}, bf16[512,4096]{1,0:T(8,128)(2,1)}) fusion(bf16[512,4096]{1,0:T(8,128)(2,1)} %fusion.44, pred[]{:T(512)S(6)} %eq.2, bf16[512,8192]{1,0:T(8,128)(2,1)} %collective-permute-done.5, bf16[8192,4096]{1,0:T(8,128)(2,1)} %param.7), kind=kOutput, calls=%fused_computation.8 | convolution fusion | flops 34363932672 | bytes 88080384 | tf_op jit(solution)/shard_map/dot_general | solution.py:30
  1292.4 66.9 %reduce-scatter.6.cloned.1.call-done = bf16[1024,1024]{1,0:T(8,128)(2,1)} async-done(((bf16[1024,4096]{1,0:T(8,128)(2,1)}), bf16[1024,1024]{1,0:T(8,128)(2,1)}) %reduce-scatter.6.cloned.1.call-update) | async-done | bytes 2097168 | tf_op jit(solution)/shard_map/reduce_scatter | solution.py:34
  (42 shorter events, 57.6 us)
Async XLA Ops:
  6.5 37.0 %all-gather.4.cloned.1.call-start = ((), (), s32[]{:S(2)}) async-start(), calls=%async_computation.3 | async-start | bytes 5242880 | tf_op jit(solution)/shard_map/all_gather | solution.py:18
  9.6 93.5 %all-gather.8.cloned.1.call-start = ((), (), s32[]{:S(2)}) async-start(), calls=%async_computation.7 | async-start | bytes 5242880 | tf_op jit(solution)/shard_map/all_gather | solution.py:18
  10.4 547.3 %all-gather.6.cloned.1.call-start = ((), (), s32[]{:S(2)}) async-start(), calls=%async_computation.5 | async-start | bytes 10485760 | tf_op jit(solution)/shard_map/all_gather | solution.py:18
  13.5 1278.8 %reduce-scatter.8.cloned.1.call-start = ((), (), s32[]{:S(2)}) async-start(), calls=%async_computation.8 | async-start | bytes 5242880 | tf_op jit(solution)/shard_map/reduce_scatter | solution.py:34
  72.6 396.0 %collective-permute-start = (bf16[256,8192]{1,0:T(8,128)(2,1)}, bf16[256,8192]{1,0:T(8,128)(2,1)}, u32[]{:S(2)}, u32[]{:S(2)}) collective-permute-start(bf16[256,8192]{1,0:T(8,128)(2,1)} %fusion.22), channel_id=1, source_target_pairs={{0,4},{4,0},{1,5},{5,1},{2,6},{6,2},{3,7},{7,3}} | collective-permute-start | bytes 12582920 | tf_op jit(solution)/shard_map/ppermute | solution.py:21
  102.9 365.7 %collective-permute-start.1 = (bf16[256,8192]{1,0:T(8,128)(2,1)}, bf16[256,8192]{1,0:T(8,128)(2,1)}, u32[]{:S(2)}, u32[]{:S(2)}) collective-permute-start(bf16[256,8192]{1,0:T(8,128)(2,1)} %fusion.20), channel_id=1, source_target_pairs={{0,4},{4,0},{1,5},{5,1},{2,6},{6,2},{3,7},{7,3}} | collective-permute-start | bytes 12582920 | tf_op jit(solution)/shard_map/ppermute | solution.py:22
  132.4 211.9 %collective-permute-start.6 = (bf16[256,8192]{1,0:T(8,128)(2,1)}, bf16[256,8192]{1,0:T(8,128)(2,1)}, u32[]{:S(2)}, u32[]{:S(2)}) collective-permute-start(bf16[256,8192]{1,0:T(8,128)(2,1)} %fusion.12), channel_id=1, source_target_pairs={{0,4},{4,0},{1,5},{5,1},{2,6},{6,2},{3,7},{7,3}} | collective-permute-start | bytes 12582920 | tf_op jit(solution)/shard_map/ppermute | solution.py:21
  162.7 271.5 %collective-permute-start.7 = (bf16[256,8192]{1,0:T(8,128)(2,1)}, bf16[256,8192]{1,0:T(8,128)(2,1)}, u32[]{:S(2)}, u32[]{:S(2)}) collective-permute-start(bf16[256,8192]{1,0:T(8,128)(2,1)} %fusion.10), channel_id=1, source_target_pairs={{0,4},{4,0},{1,5},{5,1},{2,6},{6,2},{3,7},{7,3}} | collective-permute-start | bytes 12582920 | tf_op jit(solution)/shard_map/ppermute | solution.py:22
  467.4 223.6 %collective-permute-start.8 = (bf16[256,8192]{1,0:T(8,128)(2,1)}, bf16[256,8192]{1,0:T(8,128)(2,1)}, u32[]{:S(2)}, u32[]{:S(2)}) collective-permute-start(bf16[256,8192]{1,0:T(8,128)(2,1)} %multiply_convert_fusion.1), channel_id=1, source_target_pairs={{0,4},{4,0},{1,5},{5,1},{2,6},{6,2},{3,7},{7,3}} | collective-permute-start | bytes 12582920 | tf_op jit(solution)/shard_map/ppermute | solution.py:28
  501.7 28.5 %copy-start = (bf16[256,8192]{1,0:T(8,128)(2,1)S(1)}, bf16[256,8192]{1,0:T(8,128)(2,1)}, u32[]{:S(2)}) copy-start(bf16[256,8192]{1,0:T(8,128)(2,1)} %multiply_convert_fusion.2) | copy-start | bytes 12582916
  501.7 558.3 %collective-permute-start.2 = (bf16[256,8192]{1,0:T(8,128)(2,1)}, bf16[256,8192]{1,0:T(8,128)(2,1)}, u32[]{:S(2)}, u32[]{:S(2)}) collective-permute-start(bf16[256,8192]{1,0:T(8,128)(2,1)} %multiply_convert_fusion.2), channel_id=1, source_target_pairs={{0,4},{4,0},{1,5},{5,1},{2,6},{6,2},{3,7},{7,3}} | collective-permute-start | bytes 12582920 | tf_op jit(solution)/shard_map/ppermute | solution.py:28
  601.3 227.0 %collective-permute-start.3 = (bf16[512,8192]{1,0:T(8,128)(2,1)}, bf16[512,8192]{1,0:T(8,128)(2,1)}, u32[]{:S(2)}, u32[]{:S(2)}) collective-permute-start(bf16[512,8192]{1,0:T(8,128)(2,1)} %fusion.2), channel_id=1, source_target_pairs={{0,4},{4,0},{1,5},{5,1},{2,6},{6,2},{3,7},{7,3}} | collective-permute-start | bytes 25165832 | tf_op jit(solution)/shard_map/ppermute | solution.py:21
  646.2 44.8 %copy-start.2 = (bf16[256,4096]{1,0:T(8,128)(2,1)S(1)}, bf16[256,4096]{1,0:T(8,128)(2,1)}, u32[]{:S(2)}) copy-start(bf16[256,4096]{1,0:T(8,128)(2,1)} %fusion.45) | copy-start | bytes 6291460
  646.2 361.8 %collective-permute-start.4 = (bf16[512,8192]{1,0:T(8,128)(2,1)}, bf16[512,8192]{1,0:T(8,128)(2,1)}, u32[]{:S(2)}, u32[]{:S(2)}) collective-permute-start(bf16[512,8192]{1,0:T(8,128)(2,1)} %fusion), channel_id=1, source_target_pairs={{0,4},{4,0},{1,5},{5,1},{2,6},{6,2},{3,7},{7,3}} | collective-permute-start | bytes 25165832 | tf_op jit(solution)/shard_map/ppermute | solution.py:22
  720.6 339.4 %copy-start.1 = (bf16[256,4096]{1,0:T(8,128)(2,1)S(1)}, bf16[256,4096]{1,0:T(8,128)(2,1)}, u32[]{:S(2)}) copy-start(bf16[256,4096]{1,0:T(8,128)(2,1)} %fusion.43) | copy-start | bytes 6291460
  720.6 571.8 %reduce-scatter.4.cloned.1.call-start = ((), (), s32[]{:S(2)}) async-start(), calls=%async_computation.4 | async-start | bytes 5242880 | tf_op jit(solution)/shard_map/reduce_scatter | solution.py:34
  1058.8 180.3 %collective-permute-start.5 = (bf16[512,8192]{1,0:T(8,128)(2,1)}, bf16[512,8192]{1,0:T(8,128)(2,1)}, u32[]{:S(2)}, u32[]{:S(2)}) collective-permute-start(bf16[512,8192]{1,0:T(8,128)(2,1)} %multiply_convert_fusion), channel_id=1, source_target_pairs={{0,4},{4,0},{1,5},{5,1},{2,6},{6,2},{3,7},{7,3}} | collective-permute-start | bytes 25165832 | tf_op jit(solution)/shard_map/ppermute | solution.py:28
  1089.3 269.9 %reduce-scatter.6.cloned.1.call-start = ((), (), s32[]{:S(2)}) async-start(), calls=%async_computation.6 | async-start | bytes 10485760 | tf_op jit(solution)/shard_map/reduce_scatter | solution.py:34
Sparse Core Ops, SparseCore 0:
  9.7 33.7 all-gather.3
  45.0 31.4 all-gather.7
  78.1 55.7 all-gather.5
  720.7 39.0 reduce-scatter.7
  1089.5 38.4 reduce-scatter.3
  1292.5 66.7 reduce-scatter.5

commit v2 on v0

v2 whole, which is shorter than its diff:
```python
import jax
import jax.numpy as jnp
from jax import lax
from jax.experimental import pallas as pl
from jax.experimental.pallas import tpu as pltpu
from jax.sharding import PartitionSpec as P

MESH = pl.DeviceIdType.MESH
F32 = jnp.float32
BF16 = jnp.bfloat16

U = 256
T = 256
GU, HS = 4, 4
LAG_H, LAG_Y = 3, 5
LAG_R = 6


def kernel(geom, x_ref, wg_ref, wu_ref, wd_ref, out_ref, xb, wb, wdb, own, gus, gur, hb, yacc, ysend, yrecv, yown, ost,
           xsend_sem, xrecv_sem, xloc_sem, w_sem, wd_sem, gu_send_sem, gu_recv_sem, h_send_sem, h_recv_sem,
           y_send_sem, y_recv_sem, o_sem, x_credit, gu_credit, h_credit, y_credit):
    units, pairs, nb, xcols, ocols = geom
    steps = units * pairs
    loads = pairs * (2 + (units - 2) // 2)
    dp, a, b = lax.axis_index("dp"), lax.axis_index("a"), lax.axis_index("b")
    across = (dp, 1 - a, b)

    def ahead(j):
        return (dp, a, lax.rem(b + j, nb))

    def behind(j):
        return (dp, a, lax.rem(b + nb - j, nb))

    def place(s):
        r = s - pairs
        last = s - (steps - pairs)
        head, tail = s < pairs, last >= 0
        two = 2 * pairs
        rc = jnp.maximum(r, 0)
        in_pass = lax.rem(rc, two)
        unit = jnp.where(head, 0, jnp.where(tail, units - 1, 1 + 2 * lax.div(rc, two) + lax.rem(in_pass, 2)))
        pair = jnp.where(head, s, jnp.where(tail, last, lax.div(in_pass, 2)))
        load = jnp.where(head, s, jnp.where(tail, loads - pairs + last, pairs + lax.div(rc, 2)))
        alone = jnp.logical_or(head, tail)
        first = jnp.logical_or(alone, lax.rem(rc, 2) == 0)
        final = jnp.logical_or(alone, lax.rem(rc, 2) == 1)
        return unit, pair, load, first, final

    def first_step(u):
        return 0 if u == 0 else steps - pairs if u == units - 1 else pairs + 2 * pairs * ((u - 1) // 2) + (u - 1) % 2

    def last_step(u):
        return pairs - 1 if u == 0 else steps - 1 if u == units - 1 else first_step(u) + 2 * (pairs - 1)

    def aligned(i, n):
        return pl.ds(pl.multiple_of(i * n, n), n)

    def w_copies(load, slot):
        pair = lax.rem(load, pairs)
        theirs, mine = aligned(2 * pair + 1 - a, T), aligned(2 * pair + a, T)
        return [
            pltpu.make_async_copy(ref.at[:, cols], wb.at[slot, i], w_sem.at[slot, i])
            for i, (ref, cols) in enumerate(((wg_ref, theirs), (wu_ref, theirs), (wg_ref, mine), (wu_ref, mine)))
        ]

    def wd_copy(load, slot):
        return pltpu.make_async_copy(
            wd_ref.at[aligned(lax.rem(load, pairs), 2 * T), :], wdb.at[slot], wd_sem.at[slot])

    def x_remote(u, j):
        slot = u % 4
        return pltpu.make_async_remote_copy(
            src_ref=x_ref.at[pl.ds(u * U, U), :], dst_ref=xb.at[slot, :, aligned(b, xcols)],
            send_sem=xsend_sem.at[slot, j - 1], recv_sem=xrecv_sem.at[slot, j - 1],
            device_id=ahead(j), device_id_type=MESH)

    def x_arrived(u, j):
        slot = u % 4
        return pltpu.make_async_remote_copy(
            src_ref=x_ref.at[pl.ds(u * U, U), :], dst_ref=xb.at[slot, :, aligned(lax.rem(b + nb - j, nb), xcols)],
            send_sem=xsend_sem.at[slot, j - 1], recv_sem=xrecv_sem.at[slot, j - 1],
            device_id=ahead(j), device_id_type=MESH)

    def x_local(u):
        slot = u % 4
        return pltpu.make_async_copy(
            x_ref.at[pl.ds(u * U, U), :], xb.at[slot, :, aligned(b, xcols)], xloc_sem.at[slot])

    def gu_copy(slot):
        return pltpu.make_async_remote_copy(
            src_ref=gus.at[slot], dst_ref=gur.at[slot], send_sem=gu_send_sem.at[slot], recv_sem=gu_recv_sem.at[slot],
            device_id=across, device_id_type=MESH)

    def h_copy(slot, half):
        return pltpu.make_async_remote_copy(
            src_ref=hb.at[slot, half], dst_ref=hb.at[slot, half], send_sem=h_send_sem.at[slot],
            recv_sem=h_recv_sem.at[slot], device_id=across, device_id_type=MESH)

    def y_copy(slot, j):
        return pltpu.make_async_remote_copy(
            src_ref=ysend.at[slot, j - 1], dst_ref=yrecv.at[slot, j - 1], send_sem=y_send_sem.at[slot, j - 1],
            recv_sem=y_recv_sem.at[slot, j - 1], device_id=ahead(j), device_id_type=MESH)

    def o_copy(u):
        return pltpu.make_async_copy(ost.at[u % 2], out_ref.at[pl.ds(u * U, U), :], o_sem.at[u % 2])

    def send_x(u):
        for j in range(1, nb):
            if u >= 4:
                x_remote(u - 4, j).wait_send()
                pl.semaphore_wait(x_credit.at[j - 1], 1)
            x_remote(u, j).start()
        x_local(u).start()

    def wait_x(u):
        x_local(u).wait()
        for j in range(1, nb):
            x_arrived(u, j).wait_recv()

    def free_x(u):
        if u + 4 < units:
            for j in range(1, nb):
                pl.semaphore_signal(x_credit.at[j - 1], inc=1, device_id=behind(j), device_id_type=MESH)

    def scatter_y(u):
        slot = u % 2
        for j in range(1, nb):
            if u >= 2:
                y_copy(slot, j).wait_send()
            ysend[slot, j - 1] = yacc[u % 2, :, aligned(lax.rem(b + j, nb), ocols)].astype(BF16)
        yown[slot] = yacc[u % 2, :, aligned(b, ocols)]
        for j in range(1, nb):
            if u >= 2:
                pl.semaphore_wait(y_credit.at[j - 1], 1)
            y_copy(slot, j).start()

    def sum_y(u):
        slot = u % 2
        if u >= 2:
            o_copy(u - 2).wait()
        for j in range(1, nb):
            y_copy(slot, j).wait_recv()
        total = yown[slot]
        for j in range(1, nb):
            total += yrecv[slot, j - 1].astype(F32)
        ost[slot] = total.astype(BF16)
        o_copy(u).start()
        if u + 2 < units:
            for j in range(1, nb):
                pl.semaphore_signal(y_credit.at[j - 1], inc=1, device_id=behind(j), device_id_type=MESH)

    for copy in w_copies(0, 0):
        copy.start()

    barrier = pltpu.get_barrier_semaphore()
    for peer in [across] + [ahead(j) for j in range(1, nb)]:
        pl.semaphore_signal(barrier, inc=1, device_id=peer, device_id_type=MESH)
    pl.semaphore_wait(barrier, nb)

    send_x(0)
    wd_copy(0, 0).start()
    for copy in w_copies(1, 1):
        copy.start()
    wd_copy(1, 1).start()

    def first_matmuls(s):
        unit, pair, load, first, final = place(s)
        slot, wslot, xslot = lax.rem(s, GU), lax.rem(load, 2), lax.rem(unit, 4)

        @pl.when(first)
        def _():
            for copy in w_copies(load, wslot):
                copy.wait()

        for u in range(units):
            @pl.when(s == first_step(u))
            def _():
                wait_x(u)
                if u == 0:
                    for later in range(1, min(4, units)):
                        send_x(later)

        @pl.when(s >= GU)
        def _():
            gu_copy(slot).wait_send()

        rows = xb.at[xslot]
        for i in range(2):
            gus[slot, i] = jnp.dot(rows[...], wb[wslot, i], preferred_element_type=F32).astype(BF16)

        @pl.when(s >= GU)
        def _():
            pl.semaphore_wait(gu_credit, 1)

        gu_copy(slot).start()
        for i in range(2):
            own[slot, i] = jnp.dot(rows[...], wb[wslot, 2 + i], preferred_element_type=F32)

        @pl.when(jnp.logical_and(final, load + 2 < loads))
        def _():
            for copy in w_copies(load + 2, wslot):
                copy.start()

        for u in range(units):
            @pl.when(s == last_step(u))
            def _():
                free_x(u)

    def hidden(s):
        slot, hslot = lax.rem(s, GU), lax.rem(s, HS)

        @pl.when(s >= HS)
        def _():
            h_copy(hslot, a).wait_send()

        gu_copy(slot).wait_recv()
        g = own[slot, 0] + gur[slot, 0].astype(F32)
        u = own[slot, 1] + gur[slot, 1].astype(F32)
        hb[hslot, a] = (jax.nn.silu(g) * u).astype(BF16)

        @pl.when(s + GU < steps)
        def _():
            pl.semaphore_signal(gu_credit, inc=1, device_id=across, device_id_type=MESH)

        @pl.when(s >= HS)
        def _():
            pl.semaphore_wait(h_credit, 1)

        h_copy(hslot, a).start()

    def last_matmul(s):
        unit, pair, load, first, final = place(s)
        hslot, wslot, yslot = lax.rem(s, HS), lax.rem(load, 2), lax.rem(unit, 2)

        @pl.when(first)
        def _():
            wd_copy(load, wslot).wait()

        h_copy(hslot, 1 - a).wait_recv()

        @pl.when(pair == 0)
        def _():
            yacc[yslot] = jnp.zeros_like(yacc[yslot])

        yacc[yslot] += (
            jnp.dot(hb[hslot, 0], wdb[wslot, :T], preferred_element_type=F32)
            + jnp.dot(hb[hslot, 1], wdb[wslot, T:], preferred_element_type=F32))

        @pl.when(s + HS < steps)
        def _():
            pl.semaphore_signal(h_credit, inc=1, device_id=across, device_id_type=MESH)

        @pl.when(jnp.logical_and(final, load + 2 < loads))
        def _():
            wd_copy(load + 2, wslot).start()

        for u in range(units):
            @pl.when(s == last_step(u))
            def _():
                scatter_y(u)
            if u < units - 1:
                @pl.when(s == last_step(u) + LAG_R)
                def _():
                    sum_y(u)

    @pl.loop(0, steps + LAG_Y)
    def _(s):
        @pl.when(s < steps)
        def _():
            first_matmuls(s)

        for u in range(4, units):
            @pl.when(s == last_step(u - 4) + 3)
            def _():
                send_x(u)

        @pl.when(jnp.logical_and(s >= LAG_H, s < steps + LAG_H))
        def _():
            hidden(s - LAG_H)

        @pl.when(s >= LAG_Y)
        def _():
            last_matmul(s - LAG_Y)

    sum_y(units - 1)
    for u in (units - 2, units - 1):
        o_copy(u).wait()
        for j in range(1, nb):
            y_copy(u % 2, j).wait_send()
    for u in range(units - 4, units):
        for j in range(1, nb):
            x_remote(u, j).wait_send()
    for s in range(steps - GU, steps):
        gu_copy(s % GU).wait_send()
    for s in range(steps - HS, steps):
        h_copy(s % HS, a).wait_send()


def solution(mesh):
    nb = mesh.shape["b"]

    def body(x, wg, wu, wd):
        rows, xcols = x.shape
        depth, hidden = wg.shape
        outs = wd.shape[1]
        ocols = outs // nb
        units, pairs = rows // U, hidden // (2 * T)
        geom = (units, pairs, nb, xcols, ocols)
        dma, reg = pltpu.SemaphoreType.DMA, pltpu.SemaphoreType.REGULAR
        return pl.pallas_call(
            lambda *refs: kernel(geom, *refs),
            out_shape=jax.ShapeDtypeStruct((rows, ocols), BF16),
            in_specs=[pl.BlockSpec(memory_space=pl.ANY)] * 4,
            out_specs=pl.BlockSpec(memory_space=pl.ANY),
            scratch_shapes=[
                pltpu.VMEM((4, U, depth), BF16),
                pltpu.VMEM((2, 4, depth, T), BF16),
                pltpu.VMEM((2, 2 * T, outs), BF16),
                pltpu.VMEM((GU, 2, U, T), F32),
                pltpu.VMEM((GU, 2, U, T), BF16),
                pltpu.VMEM((GU, 2, U, T), BF16),
                pltpu.VMEM((HS, 2, U, T), BF16),
                pltpu.VMEM((2, U, outs), F32),
                pltpu.VMEM((2, nb - 1, U, ocols), BF16),
                pltpu.VMEM((2, nb - 1, U, ocols), BF16),
                pltpu.VMEM((2, U, ocols), F32),
                pltpu.VMEM((2, U, ocols), BF16),
                dma((4, nb - 1)), dma((4, nb - 1)), dma((4,)),
                dma((2, 4)), dma((2,)),
                dma((GU,)), dma((GU,)), dma((HS,)), dma((HS,)),
                dma((2, nb - 1)), dma((2, nb - 1)), dma((2,)),
                reg((nb - 1,)), reg, reg, reg((nb - 1,)),
            ],
            compiler_params=pltpu.CompilerParams(
                collective_id=0, has_side_effects=True, vmem_limit_bytes=67043328),
            cost_estimate=pl.CostEstimate(
                flops=6 * rows * depth * hidden, bytes_accessed=10 * depth * hidden * 3, transcendentals=rows * hidden),
            name="gated_mlp",
        )(x, wg, wu, wd)

    return jax.shard_map(
        body,
        mesh=mesh,
        in_specs=(P("dp", ("a", "b")), P("a", "b"), P("a", "b"), P("b", "a")),
        out_specs=P("dp", ("a", "b")),
        check_vma=False,
    )
```

time: 2170 us -> 1120 us (0.52)
  waiting for transfers between devices: 1680 us -> 0 us
  Pallas kernels: 0 us -> 1120 us
  matrix products: 470 us -> 0 us
    dot_general x1 -> x0, waiting for transfers between devices: 1450 us -> none  [step(): gate, up = (jnp.dot(x, w_gate), jnp.dot(x, w_up))]
    pallas_call x0 -> x1, Pallas kernels: none -> 1120 us  [body(): pl.pallas_call(lambda *refs: kernel(geom, *refs), out_shape=jax.ShapeDtyp...]
    dot_general x3 -> x0, matrix products: 470 us -> none  [the longest x2 312 us: step(): gate, up = (jnp.dot(x, w_gate), jnp.dot(x, w_up))]
    unnamed x5 -> x0, waiting for transfers between devices: 230 us -> none
  transfers between devices with their start and end apart: 3 -> 0, of which waited for: 3 -> 0; matrix products, arithmetic and copies ran while one was open for 0% -> 0% of each run, Pallas kernels for 0% -> 0%
where the time goes in v2:
time: 1120 us
  Pallas kernels  1120 us (100%)
    pallas_call x1, Pallas kernels, body(): pl.pallas_call(lambda *refs: kernel(geom, *refs), out_shape=jax.ShapeDtyp...  1120 us

profile of v2, /device:TPU:1, one launch (start us, length us, event | category | flops | bytes accessed | tf_op | source)
XLA Modules:
  0.0 1122.3 jit_solution(11257110119853088157)
XLA Ops:
  0.0 1117.6 %gated_mlp.1 = bf16[2048,1024]{1,0:T(8,128)(2,1)} custom-call(bf16[2048,1024]{1,0:T(8,128)(2,1)} %refs_0_.1, bf16[4096,8192]{1,0:T(8,128)(2,1)} %refs_1_.1, bf16[4096,8192]{1,0:T(8,128)(2,1)} %refs_2_.1, bf16[8192,4096]{1,0:T(8,128)(2,1)} %refs_3_.1), custom_call_target="tpu_custom_call" | custom-call | flops 412316860416 | bytes 1006632960 | tf_op jit(solution)/shard_map/gated_mlp/pallas_call | solution.py:310
  1117.6 4.6 copy.6

commit v3 on v2

--- a/solution.py
+++ b/solution.py
@@ -9,7 +9,7 @@
 F32 = jnp.float32
 BF16 = jnp.bfloat16
 
-U = 256
+U = 128
 T = 256
 GU, HS = 4, 4
 LAG_H, LAG_Y = 3, 5
@@ -136,15 +136,12 @@
 
     def sum_y(u):
         slot = u % 2
-        if u >= 2:
-            o_copy(u - 2).wait()
         for j in range(1, nb):
             y_copy(slot, j).wait_recv()
         total = yown[slot]
         for j in range(1, nb):
             total += yrecv[slot, j - 1].astype(F32)
-        ost[slot] = total.astype(BF16)
-        o_copy(u).start()
+        out_ref[pl.ds(u * U, U), :] = total.astype(BF16)
         if u + 2 < units:
             for j in range(1, nb):
                 pl.semaphore_signal(y_credit.at[j - 1], inc=1, device_id=behind(j), device_id_type=MESH)
@@ -176,9 +173,6 @@
             @pl.when(s == first_step(u))
             def _():
                 wait_x(u)
-                if u == 0:
-                    for later in range(1, min(4, units)):
-                        send_x(later)
 
         @pl.when(s >= GU)
         def _():
@@ -269,8 +263,8 @@
         def _():
             first_matmuls(s)
 
-        for u in range(4, units):
-            @pl.when(s == last_step(u - 4) + 3)
+        for u in range(1, units):
+            @pl.when(s == (2 * u if u < 4 else last_step(u - 4) + 3))
             def _():
                 send_x(u)
 
@@ -284,7 +278,6 @@
 
     sum_y(units - 1)
     for u in (units - 2, units - 1):
-        o_copy(u).wait()
         for j in range(1, nb):
             y_copy(u % 2, j).wait_send()
     for u in range(units - 4, units):
@@ -309,9 +302,9 @@
         dma, reg = pltpu.SemaphoreType.DMA, pltpu.SemaphoreType.REGULAR
         return pl.pallas_call(
             lambda *refs: kernel(geom, *refs),
-            out_shape=jax.ShapeDtypeStruct((rows, ocols), BF16),
+            out_shape=pltpu.VMEM((rows, ocols), BF16),
             in_specs=[pl.BlockSpec(memory_space=pl.ANY)] * 4,
-            out_specs=pl.BlockSpec(memory_space=pl.ANY),
+            out_specs=pl.BlockSpec(memory_space=pltpu.VMEM),
             scratch_shapes=[
                 pltpu.VMEM((4, U, depth), BF16),
                 pltpu.VMEM((2, 4, depth, T), BF16),
@@ -332,7 +325,7 @@
                 reg((nb - 1,)), reg, reg, reg((nb - 1,)),
             ],
             compiler_params=pltpu.CompilerParams(
-                collective_id=0, has_side_effects=True, vmem_limit_bytes=67043328),
+                collective_id=0, has_side_effects=True, vmem_limit_bytes=58 * 1024 * 1024),
             cost_estimate=pl.CostEstimate(
                 flops=6 * rows * depth * hidden, bytes_accessed=10 * depth * hidden * 3, transcendentals=rows * hidden),
             name="gated_mlp",

time: 1120 us -> 1110 us (level)
  no operation moved by 1% of the time
where the time goes in v3:
time: 1110 us
  Pallas kernels  1110 us (100%)
    pallas_call x1, Pallas kernels, body(): pl.pallas_call(lambda *refs: kernel(geom, *refs), out_shape=pltpu.VMEM((r...  1110 us

profile of v3, /device:TPU:1, one launch (start us, length us, event | category | flops | bytes accessed | tf_op | source)
XLA Modules:
  0.0 1110.9 jit_solution(4688767915007748416)
XLA Ops:
  0.0 1108.9 %gated_mlp.1 = bf16[2048,1024]{1,0:T(8,128)(2,1)S(1)} custom-call(bf16[2048,1024]{1,0:T(8,128)(2,1)} %refs_0_.1, bf16[4096,8192]{1,0:T(8,128)(2,1)} %refs_1_.1, bf16[4096,8192]{1,0:T(8,128)(2,1)} %refs_2_.1, bf16[8192,4096]{1,0:T(8,128)(2,1)} %refs_3_.1), custom_call_target="tpu_custom_call" | custom-call | flops 412316860416 | bytes 1006632960 | tf_op jit(solution)/shard_map/gated_mlp/pallas_call | solution.py:303
  1108.9 2.0 copy.6

commit v4 on v3

--- a/solution.py
+++ b/solution.py
@@ -13,7 +13,7 @@
 T = 256
 GU, HS = 4, 4
 LAG_H, LAG_Y = 3, 5
-LAG_R = 6
+LAG_R = 13
 
 
 def kernel(geom, x_ref, wg_ref, wu_ref, wd_ref, out_ref, xb, wb, wdb, own, gus, gur, hb, yacc, ysend, yrecv, yown, ost,

time: 1110 us -> 1110 us (level)
  no operation moved by 1% of the time
where the time goes in v4:
time: 1110 us
  Pallas kernels  1110 us (100%)
    pallas_call x1, Pallas kernels, body(): pl.pallas_call(lambda *refs: kernel(geom, *refs), out_shape=pltpu.VMEM((r...  1110 us

profile of v4, /device:TPU:1, one launch (start us, length us, event | category | flops | bytes accessed | tf_op | source)
XLA Modules:
  0.0 1110.1 jit_solution(6007811439170144977)
XLA Ops:
  0.0 1108.0 %gated_mlp.1 = bf16[2048,1024]{1,0:T(8,128)(2,1)S(1)} custom-call(bf16[2048,1024]{1,0:T(8,128)(2,1)} %refs_0_.1, bf16[4096,8192]{1,0:T(8,128)(2,1)} %refs_1_.1, bf16[4096,8192]{1,0:T(8,128)(2,1)} %refs_2_.1, bf16[8192,4096]{1,0:T(8,128)(2,1)} %refs_3_.1), custom_call_target="tpu_custom_call" | custom-call | flops 412316860416 | bytes 1006632960 | tf_op jit(solution)/shard_map/gated_mlp/pallas_call | solution.py:303
  1108.1 2.0 copy.6

commit v5 on v4

--- a/solution.py
+++ b/solution.py
@@ -122,17 +122,31 @@
             for j in range(1, nb):
                 pl.semaphore_signal(x_credit.at[j - 1], inc=1, device_id=behind(j), device_id_type=MESH)
 
-    def scatter_y(u):
-        slot = u % 2
-        for j in range(1, nb):
-            if u >= 2:
+    def scatter_y(unit, finish):
+        slot = lax.rem(unit, 2)
+        dests = (1, 2, 3)
+
+        def block(j):
+            cols = aligned(lax.rem(b + j, nb), ocols)
+            return yacc[slot, :, cols] + finish(cols)
+
+        for i, j in enumerate(dests):
+            @pl.when(unit >= 2)
+            def _():
                 y_copy(slot, j).wait_send()
-            ysend[slot, j - 1] = yacc[u % 2, :, aligned(lax.rem(b + j, nb), ocols)].astype(BF16)
-        yown[slot] = yacc[u % 2, :, aligned(b, ocols)]
-        for j in range(1, nb):
-            if u >= 2:
-                pl.semaphore_wait(y_credit.at[j - 1], 1)
-            y_copy(slot, j).start()
+
+            ysend[slot, j - 1] = block(j).astype(BF16)
+            if i:
+                start_y(unit, slot, dests[i - 1])
+        yown[slot] = block(0)
+        start_y(unit, slot, dests[-1])
+
+    def start_y(unit, slot, j):
+        @pl.when(unit >= 2)
+        def _():
+            pl.semaphore_wait(y_credit.at[j - 1], 1)
+
+        y_copy(slot, j).start()
 
     def sum_y(u):
         slot = u % 2
@@ -230,15 +244,23 @@
         def _():
             wd_copy(load, wslot).wait()
 
+        @pl.when(pair == 0)
+        def _():
+            yacc[yslot] = jnp.zeros_like(yacc[yslot])
+
+        yacc[yslot] += jnp.dot(hb[hslot, a], wdb[wslot, aligned(a, T)], preferred_element_type=F32)
         h_copy(hslot, 1 - a).wait_recv()
 
-        @pl.when(pair == 0)
-        def _():
-            yacc[yslot] = jnp.zeros_like(yacc[yslot])
-
-        yacc[yslot] += (
-            jnp.dot(hb[hslot, 0], wdb[wslot, :T], preferred_element_type=F32)
-            + jnp.dot(hb[hslot, 1], wdb[wslot, T:], preferred_element_type=F32))
+        def theirs(cols):
+            return jnp.dot(hb[hslot, 1 - a], wdb[wslot, aligned(1 - a, T), cols], preferred_element_type=F32)
+
+        @pl.when(pair < pairs - 1)
+        def _():
+            yacc[yslot] += theirs(slice(None))
+
+        @pl.when(pair == pairs - 1)
+        def _():
+            scatter_y(unit, theirs)
 
         @pl.when(s + HS < steps)
         def _():
@@ -249,9 +271,6 @@
             wd_copy(load + 2, wslot).start()
 
         for u in range(units):
-            @pl.when(s == last_step(u))
-            def _():
-                scatter_y(u)
             if u < units - 1:
                 @pl.when(s == last_step(u) + LAG_R)
                 def _():

time: 1110 us -> 1110 us (level)
  no operation moved by 1% of the time
where the time goes in v5:
time: 1110 us
  Pallas kernels  1110 us (100%)
    pallas_call x1, Pallas kernels, body(): pl.pallas_call(lambda *refs: kernel(geom, *refs), out_shape=pltpu.VMEM((r...  1110 us

profile of v5, /device:TPU:1, one launch (start us, length us, event | category | flops | bytes accessed | tf_op | source)
XLA Modules:
  0.0 1109.9 jit_solution(5602151317322392327)
XLA Ops:
  0.0 1107.9 %gated_mlp.1 = bf16[2048,1024]{1,0:T(8,128)(2,1)S(1)} custom-call(bf16[2048,1024]{1,0:T(8,128)(2,1)} %refs_0_.1, bf16[4096,8192]{1,0:T(8,128)(2,1)} %refs_1_.1, bf16[4096,8192]{1,0:T(8,128)(2,1)} %refs_2_.1, bf16[8192,4096]{1,0:T(8,128)(2,1)} %refs_3_.1), custom_call_target="tpu_custom_call" | custom-call | flops 412316860416 | bytes 1006632960 | tf_op jit(solution)/shard_map/gated_mlp/pallas_call | solution.py:322
  1107.9 2.0 copy.6
